TPU v7x, 256 devices: a whole 4x4x8 slice. The times are simulated.
256 devices in a mesh: unit: 4 (over y), bank: 4 (over x), zero: 16 (over z, core).
Axes of the slice: x: 4, y: 4, z: 8, core: 2. Of those that a mesh axis runs over, the one named last changes fastest.
Arguments:
- train_down: float32 [256, 1024, 2048], P(('unit', 'bank'), None, 'zero'), parts along dimension 0, may hold values from -0.25 to 0.25
- router_weight: float32 [8192, 64], P(('unit', 'zero'), 'bank'), parts along dimension 0, may hold values from -0.125 to 0.125
- router_gain: float32 [8192], P(('unit', 'zero')), parts along dimension 0, may hold values from 0.25 to 1.75
Outputs:
- ready_down: bfloat16 [256, 1024, 2048], P(('unit', 'bank'), 'zero'), parts along dimension 0
- scale_down: float32 [256, 1024], P(('unit', 'bank'), 'zero'), parts along dimension 0
- serve_router: bfloat16 [8192, 64], P('unit'), parts along dimension 0
There are 4 independent parts, one for each index of `unit`. A program takes and returns all parts, laid end to end along the dimension named above; each array names one. Nothing has to cross between parts.
All inputs are finite; a program needn't handle non-finite values.
Results may differ from a plain program's by a relative error of at most 0.001.
Values may be sent and summed in bfloat16 or wider, within the bound.
A program may use at most 128 MiB of HBM per device.

v0:
```python
import jax
import jax.numpy as jnp
from jax import lax
from jax.sharding import Mesh
from jax.sharding import PartitionSpec as P

ZERO = ("zero_0", "zero_1")
UNIT_ZERO = ("unit", "zero_0", "zero_1")


def gathered_total(value, axis):
    tiles = lax.all_gather(value, axis)
    return tiles.max(axis=0)


def in_blocks(value, dim, length):
    return jnp.stack(jnp.split(value, length, axis=dim))


def joined_along(tiles, dim):
    tiles = jnp.moveaxis(tiles, 0, dim)
    dims = tiles.shape
    return tiles.reshape(*dims[:dim], dims[dim] * dims[dim + 1], *dims[dim + 2 :])


def turned_blocks(tiles, axes, sequence):
    dims = [lax.axis_size(a) for a in axes]
    tiles = tiles.reshape(*dims, *tiles.shape[1:])
    for k in sequence:
        tiles = lax.all_to_all(tiles, axes[k], split_axis=k, concat_axis=k, tiled=True)
    return tiles.reshape(-1, *tiles.shape[len(axes) :])


def two_step_exchange(value, groups, sequence, split_dim, concat_dim):
    length = lax.axis_size(groups[0]) * lax.axis_size(groups[1])
    tiles = in_blocks(value, split_dim, length)
    return joined_along(turned_blocks(tiles, groups, sequence), concat_dim)


def per_device(train_down, router_weight, router_gain):
    scale_down = gathered_total(jnp.max(jnp.abs(train_down), axis=2), ZERO)
    narrow_down = (train_down / jnp.expand_dims(scale_down, 2)).astype(jnp.bfloat16)
    ready_down = two_step_exchange(narrow_down, ("zero_0", "zero_1"), (1, 0), 1, 2)
    scale_down = lax.dynamic_slice_in_dim(
        scale_down, lax.axis_index(ZERO) * ready_down.shape[1], ready_down.shape[1], axis=1
    )
    part_router = (router_weight * router_gain[:, None]).astype(jnp.bfloat16)
    row_router = lax.all_gather(part_router, ZERO, axis=0, tiled=True)
    serve_router = lax.all_gather(row_router, "bank", axis=1, tiled=True)
    return (ready_down, scale_down, serve_router)


def solution(mesh):
    torus = Mesh(
        mesh.devices.reshape(mesh.shape["unit"], mesh.shape["bank"], 8, 2),
        ("unit", "bank", "zero_0", "zero_1"),
    )
    placed = (P(("unit", "bank"), None, ZERO), P(UNIT_ZERO, "bank"), P(UNIT_ZERO))
    return jax.shard_map(
        per_device,
        mesh=torus,
        in_specs=placed,
        out_specs=(P(("unit", "bank"), ZERO, None), P(("unit", "bank"), ZERO), P("unit", None)),
        check_vma=False,
    )
```

profile of v0, /device:TPU:2, one launch (start us, length us, event | category | flops | bytes accessed | tf_op | source)
XLA Modules:
  0.0 208.9 jit_solution(14406718394577058157)
XLA Ops:
  7.2 0.0 all-gather.3.cloned.1.call-start
  7.2 6.2 %abs_reduce_fusion = f32[16,1024]{1,0:T(8,128)} fusion(f32[16,1024,128]{2,1,0:T(8,128)} %param.3), kind=kLoop, calls=%fused_computation.1 | loop fusion | flops 4177920 | bytes 8454144 | tf_op jit(solution)/shard_map/reduce_max | solution.py:41
  13.5 0.0 all-gather.3.cloned.1.call-update
  13.5 41.7 %all-gather.3.cloned.1.call-done = f32[256,1024]{1,0:T(8,128)} async-done(((f32[16,1024]{1,0:T(8,128)}), f32[256,1024]{1,0:T(8,128)}) %all-gather.3.cloned.1.call-update) | async-done | bytes 1048592 | tf_op jit(solution)/shard_map/all_gather | solution.py:12
  55.1 1.3 reduce_max.19
  56.4 5.3 %divide_convert_fusion = bf16[16,1024,128]{2,1,0:T(8,128)(2,1)S(1)} fusion(f32[16,1024,128]{2,1,0:T(8,128)} %param.3, f32[16,1024]{1,0:T(8,128)S(1)} %reduce_max.19), kind=kLoop, calls=%fused_computation | loop fusion | flops 4194304 | bytes 12648448 | tf_op jit(solution)/shard_map/convert_element_type | solution.py:42
  62.4 1.3 copy.12
  63.7 7.1 %all_to_all.10 = bf16[8,2,16,64,128]{4,3,2,0,1:T(8,128)(2,1)S(1)} all-to-all(bf16[8,2,16,64,128]{4,3,2,0,1:T(8,128)(2,1)S(1)} %copy.12), channel_id=1, replica_groups=mesh['unit'=4,'bank'=4,'zero_0'=8,'zero_1'=2] {'zero_1'}, dimensions={1} | all-to-all | bytes 8388608 | tf_op jit(solution)/shard_map/all_to_all | solution.py:30
  70.8 3.0 %copy.13 = bf16[8,2,16,64,128]{4,3,2,1,0:T(8,128)(2,1)} copy(bf16[8,2,16,64,128]{4,3,2,0,1:T(8,128)(2,1)S(1)} %all_to_all.10) | data formatting | bytes 8388608 | tf_op jit(solution)/shard_map/all_to_all | solution.py:30
  73.8 0.0 copy-start
  73.8 0.0 copy-start.1
  73.8 4.7 %all-to-all-start.1 = ((bf16[8,2,16,64,128]{4,3,2,1,0:T(8,128)(2,1)}), bf16[8,2,16,64,128]{4,3,2,1,0:T(8,128)(2,1)}, u32[]{:S(2)}, u32[]{:S(2)}) async-start(bf16[8,2,16,64,128]{4,3,2,1,0:T(8,128)(2,1)} %copy.13), calls=%async_computation.1 | async-start | bytes 8388608 | tf_op jit(solution)/shard_map/all_to_all | solution.py:30
  78.5 0.0 copy-done
  78.5 0.0 copy-done.1
  78.5 104.4 %all_gather.14 = bf16[2048,16]{0,1:T(8,128)(2,1)S(1)} all-gather(bf16[128,16]{0,1:T(8,128)(2,1)S(1)} %multiply_convert_fusion), channel_id=1, replica_groups=mesh['unit'=4,'bank'=4,'zero_0'=8,'zero_1'=2] {'zero_0','zero_1'}, dimensions={0}, use_global_device_ids=true | all-gather | bytes 69632 | tf_op jit(solution)/shard_map/all_gather | solution.py:48
  182.9 12.5 %all_gather.15 = bf16[2048,64]{0,1:T(8,128)(2,1)S(1)} all-gather(bf16[2048,16]{0,1:T(8,128)(2,1)S(1)} %all_gather.14), channel_id=1, replica_groups=mesh['unit'=4,'bank'=4,'zero_0'=8,'zero_1'=2] {'bank'}, dimensions={1}, use_global_device_ids=true | all-gather | bytes 327680 | tf_op jit(solution)/shard_map/all_gather | solution.py:49
  195.4 0.7 constant_dynamic-slice_fusion
  196.0 0.0 all-to-all-done.1
  196.0 5.3 %copy.17 = bf16[16,16,8,8,128]{4,3,0,2,1:T(8,128)(2,1)} copy(bf16[16,16,8,8,128]{4,3,2,1,0:T(8,128)(2,1)} %bitcast.21) | data formatting | bytes 8388608 | tf_op jit(solution)/shard_map/reshape | solution.py:23
  201.4 0.7 copy.34
  (17 shorter events, 0.6 us)
Async XLA Ops:
  7.2 48.0 %all-gather.3.cloned.1.call-start = ((), (), s32[]{:S(2)}) async-start(), calls=%async_computation.2 | async-start | bytes 1114112 | tf_op jit(solution)/shard_map/all_gather | solution.py:12
  73.8 4.7 %copy-start = (f32[128,16]{0,1:T(8,128)S(1)}, f32[128,16]{0,1:T(8,128)}, u32[]{:S(2)}) copy-start(f32[128,16]{0,1:T(8,128)} %param.4) | copy-start | bytes 24580
  73.8 4.7 %copy-start.1 = (f32[128]{0:T(128)S(1)}, f32[128]{0:T(128)}, u32[]{:S(2)}) copy-start(f32[128]{0:T(128)} %param.5) | copy-start | bytes 1540
  73.8 122.2 %all-to-all-start.1 = ((bf16[8,2,16,64,128]{4,3,2,1,0:T(8,128)(2,1)}), bf16[8,2,16,64,128]{4,3,2,1,0:T(8,128)(2,1)}, u32[]{:S(2)}, u32[]{:S(2)}) async-start(bf16[8,2,16,64,128]{4,3,2,1,0:T(8,128)(2,1)} %copy.13), calls=%async_computation.1 | async-start | bytes 8388608 | tf_op jit(solution)/shard_map/all_to_all | solution.py:30
Sparse Core Ops, SparseCore 0:
  13.6 41.4 all-gather.2
where the time goes:
time: 209 us
  blocking collectives  124 us (59%)
  waiting for transfers between devices  41.7 us (20%)
  between operations  14.2 us (7%)
  other arithmetic  12.8 us (6%)
  local copies, waits for them, and re-layouts  11.6 us (6%)
  starting transfers between devices  4.71 us (2%)
    all_gather x1, blocking collectives, per_device(): row_router = lax.all_gather(part_router, ZERO, axis=0, tiled=True)  104 us
    all_gather x1, waiting for transfers between devices, gathered_total(): tiles = lax.all_gather(value, axis)  41.7 us
    all_gather x1, blocking collectives, per_device(): serve_router = lax.all_gather(row_router, 'bank', axis=1, tiled=True)  12.5 us
    all_to_all x1, blocking collectives, turned_blocks(): lax.all_to_all(tiles, axes[k], split_axis=k, concat_axis=k, tiled=True)  7.1 us
    reduce_max x1, other arithmetic, per_device(): scale_down = gathered_total(jnp.max(jnp.abs(train_down), axis=2), ZERO)  6.25 us
    reshape x1, local copies, waits for them, and re-layouts, joined_along(): tiles.reshape(*dims[:dim], dims[dim] * dims[dim + 1], *dims[dim + 2:])  5.35 us
    convert_element_type x1, other arithmetic, per_device(): (train_down / jnp.expand_dims(scale_down, 2)).astype(jnp.bfloat16)  5.26 us
    all_to_all x1, starting transfers between devices, turned_blocks(): lax.all_to_all(tiles, axes[k], split_axis=k, concat_axis=k, tiled=True)  4.67 us
  transfers between devices with their start and end apart: 2, of which 1 were waited for; matrix products, arithmetic and copies ran while one was open for 0% of the time, Pallas kernels for 0%

commit v1 on v0

--- a/solution.py
+++ b/solution.py
@@ -46,7 +46,11 @@
     )
     part_router = (router_weight * router_gain[:, None]).astype(jnp.bfloat16)
     row_router = lax.all_gather(part_router, ZERO, axis=0, tiled=True)
-    serve_router = lax.all_gather(row_router, "bank", axis=1, tiled=True)
+    devices = lax.axis_size("bank")
+    repeats = [devices if d == 1 else 1 for d in range(row_router.ndim)]
+    serve_router = lax.all_to_all(
+        jnp.tile(row_router, repeats), "bank", split_axis=1, concat_axis=1, tiled=True
+    )
     return (ready_down, scale_down, serve_router)
 
 

time: 209 us -> 198 us (0.947)
  blocking collectives: 124 us -> 28.3 us
  waiting for transfers between devices: 41.7 us -> 117 us
  starting transfers between devices: 4.71 us -> 9.39 us
  local copies, waits for them, and re-layouts: 11.6 us -> 14.8 us
    all_to_all x1, waiting for transfers between devices: 0.01 us -> 95.6 us  [turned_blocks(): lax.all_to_all(tiles, axes[k], split_axis=k, concat_axis=k, tiled=True)]
    all_gather x1, blocking collectives: 104 us -> 20.1 us  [per_device(): row_router = lax.all_gather(part_router, ZERO, axis=0, tiled=True)]
    all_gather x1, waiting for transfers between devices: 41.7 us -> 21.5 us  [gathered_total(): tiles = lax.all_gather(value, axis)]
    all_gather x1 -> x0, blocking collectives: 12.5 us -> none  [per_device(): serve_router = lax.all_gather(row_router, 'bank', axis=1, tiled=True)]
    all_to_all x0 -> x1, starting transfers between devices: none -> 4.8 us  [per_device(): lax.all_to_all(jnp.tile(row_router, repeats), 'bank', split_axis=1, conca...]
    all_to_all x1, local copies, waits for them, and re-layouts: 2.97 us -> 5.52 us  [turned_blocks(): lax.all_to_all(tiles, axes[k], split_axis=k, concat_axis=k, tiled=True)]
  transfers between devices with their start and end apart: 2 -> 3, of which waited for: 1 -> 2; matrix products, arithmetic and copies ran while one was open for 0% -> 3% of each run, Pallas kernels for 0% -> 0%
where the time goes in v1:
time: 198 us; the launch traced here: 197 us
  waiting for transfers between devices  117 us (59%)
  blocking collectives  28.3 us (14%)
  local copies, waits for them, and re-layouts  14.8 us (7%)
  between operations  14.2 us (7%)
  other arithmetic  12.8 us (6%)
  starting transfers between devices  9.39 us (5%)
    all_to_all x1, waiting for transfers between devices, turned_blocks(): lax.all_to_all(tiles, axes[k], split_axis=k, concat_axis=k, tiled=True)  95.6 us
    all_gather x1, waiting for transfers between devices, gathered_total(): tiles = lax.all_gather(value, axis)  21.5 us
    all_gather x1, blocking collectives, per_device(): row_router = lax.all_gather(part_router, ZERO, axis=0, tiled=True)  20.1 us
    all_to_all x1, blocking collectives, turned_blocks(): lax.all_to_all(tiles, axes[k], split_axis=k, concat_axis=k, tiled=True)  8.15 us
    reduce_max x1, other arithmetic, per_device(): scale_down = gathered_total(jnp.max(jnp.abs(train_down), axis=2), ZERO)  6.25 us
    all_to_all x1, local copies, waits for them, and re-layouts, turned_blocks(): lax.all_to_all(tiles, axes[k], split_axis=k, concat_axis=k, tiled=True)  5.52 us
    reshape x1, local copies, waits for them, and re-layouts, joined_along(): tiles.reshape(*dims[:dim], dims[dim] * dims[dim + 1], *dims[dim + 2:])  5.35 us
    convert_element_type x1, other arithmetic, per_device(): (train_down / jnp.expand_dims(scale_down, 2)).astype(jnp.bfloat16)  5.26 us
  transfers between devices with their start and end apart: 3, of which 2 were waited for; matrix products, arithmetic and copies ran while one was open for 3% of the time, Pallas kernels for 0%

profile of v1, /device:TPU:2, one launch (start us, length us, event | category | flops | bytes accessed | tf_op | source)
XLA Modules:
  0.0 196.6 jit_solution(3755257042915347789)
XLA Ops:
  7.2 0.0 copy-start
  7.2 0.0 copy-start.1
  7.2 0.0 all-gather.3.cloned.1.call-start
  7.2 6.2 %abs_reduce_fusion = f32[16,1024]{1,0:T(8,128)} fusion(f32[16,1024,128]{2,1,0:T(8,128)} %param.3), kind=kLoop, calls=%fused_computation.1 | loop fusion | flops 4177920 | bytes 8454144 | tf_op jit(solution)/shard_map/reduce_max | solution.py:41
  13.5 0.0 all-gather.3.cloned.1.call-update
  13.5 0.0 copy-done
  13.5 0.0 copy-done.1
  13.5 20.1 %all_gather.11 = bf16[2048,16]{0,1:T(8,128)(2,1)S(1)} all-gather(bf16[128,16]{0,1:T(8,128)(2,1)S(1)} %multiply_convert_fusion), channel_id=1, replica_groups=mesh['unit'=4,'bank'=4,'zero_0'=8,'zero_1'=2] {'zero_0','zero_1'}, dimensions={0}, use_global_device_ids=true | all-gather | bytes 69632 | tf_op jit(solution)/shard_map/all_gather | solution.py:48
  33.7 21.5 %all-gather.3.cloned.1.call-done = f32[256,1024]{1,0:T(8,128)} async-done(((f32[16,1024]{1,0:T(8,128)}), f32[256,1024]{1,0:T(8,128)}) %all-gather.3.cloned.1.call-update) | async-done | bytes 1048592 | tf_op jit(solution)/shard_map/all_gather | solution.py:12
  55.2 1.3 reduce_max.19
  56.5 5.3 %divide_convert_fusion = bf16[16,1024,128]{2,1,0:T(8,128)(2,1)S(1)} fusion(f32[16,1024,128]{2,1,0:T(8,128)} %param.3, f32[16,1024]{1,0:T(8,128)S(1)} %reduce_max.19), kind=kLoop, calls=%fused_computation | loop fusion | flops 4194304 | bytes 12648448 | tf_op jit(solution)/shard_map/convert_element_type | solution.py:42
  62.4 1.3 copy.12
  63.7 8.2 %all_to_all.19 = bf16[8,2,16,64,128]{4,3,2,0,1:T(8,128)(2,1)} all-to-all(bf16[8,2,16,64,128]{4,3,2,0,1:T(8,128)(2,1)S(1)} %copy.12), channel_id=1, replica_groups=mesh['unit'=4,'bank'=4,'zero_0'=8,'zero_1'=2] {'zero_1'}, dimensions={1} | all-to-all | bytes 8388608 | tf_op jit(solution)/shard_map/all_to_all | solution.py:30
  71.9 0.7 tile.2
  72.6 4.8 %all-to-all-start.2 = ((bf16[2048,4,16]{0,2,1:T(8,128)(2,1)}), bf16[2048,4,16]{0,2,1:T(8,128)(2,1)S(1)}, u32[]{:S(2)}, u32[]{:S(2)}) async-start(bf16[2048,4,16]{0,2,1:T(8,128)(2,1)} %tile.2), calls=%async_computation.2 | async-start | bytes 524288 | tf_op jit(solution)/shard_map/all_to_all | solution.py:51
  77.4 5.5 %copy.13 = bf16[8,2,16,64,128]{4,3,2,1,0:T(8,128)(2,1)} copy(bf16[8,2,16,64,128]{4,3,2,0,1:T(8,128)(2,1)} %all_to_all.19) | data formatting | bytes 8388608 | tf_op jit(solution)/shard_map/all_to_all | solution.py:30
  82.9 0.0 all-to-all-done.2
  82.9 4.5 %all-to-all-start.1 = ((bf16[8,2,16,64,128]{4,3,2,1,0:T(8,128)(2,1)}), bf16[8,2,16,64,128]{4,3,2,1,0:T(8,128)(2,1)}, u32[]{:S(2)}, u32[]{:S(2)}) async-start(bf16[8,2,16,64,128]{4,3,2,1,0:T(8,128)(2,1)} %copy.13), calls=%async_computation.1 | async-start | bytes 8388608 | tf_op jit(solution)/shard_map/all_to_all | solution.py:30
  87.5 0.7 constant_dynamic-slice_fusion
  88.2 95.6 %all-to-all-done.1 = bf16[8,2,16,64,128]{4,3,2,1,0:T(8,128)(2,1)} async-done(((bf16[8,2,16,64,128]{4,3,2,1,0:T(8,128)(2,1)}), bf16[8,2,16,64,128]{4,3,2,1,0:T(8,128)(2,1)}, u32[]{:S(2)}, u32[]{:S(2)}) %all-to-all-start.1) | async-done | bytes 4194336 | tf_op jit(solution)/shard_map/all_to_all | solution.py:30
  183.7 5.3 %copy.17 = bf16[16,16,8,8,128]{4,3,0,2,1:T(8,128)(2,1)} copy(bf16[16,16,8,8,128]{4,3,2,1,0:T(8,128)(2,1)} %bitcast.22) | data formatting | bytes 8388608 | tf_op jit(solution)/shard_map/reshape | solution.py:23
  189.1 0.7 copy.34
  (17 shorter events, 0.6 us)
Async XLA Ops:
  7.2 6.3 %copy-start = (f32[128,16]{0,1:T(8,128)S(1)}, f32[128,16]{0,1:T(8,128)}, u32[]{:S(2)}) copy-start(f32[128,16]{0,1:T(8,128)} %param.4) | copy-start | bytes 24580
  7.2 6.3 %copy-start.1 = (f32[128]{0:T(128)S(1)}, f32[128]{0:T(128)}, u32[]{:S(2)}) copy-start(f32[128]{0:T(128)} %param.5) | copy-start | bytes 1540
  7.2 48.0 %all-gather.3.cloned.1.call-start = ((), (), s32[]{:S(2)}) async-start(), calls=%async_computation.3 | async-start | bytes 1114112 | tf_op jit(solution)/shard_map/all_gather | solution.py:12
  72.6 10.3 %all-to-all-start.2 = ((bf16[2048,4,16]{0,2,1:T(8,128)(2,1)}), bf16[2048,4,16]{0,2,1:T(8,128)(2,1)S(1)}, u32[]{:S(2)}, u32[]{:S(2)}) async-start(bf16[2048,4,16]{0,2,1:T(8,128)(2,1)} %tile.2), calls=%async_computation.2 | async-start | bytes 524288 | tf_op jit(solution)/shard_map/all_to_all | solution.py:51
  82.9 100.8 %all-to-all-start.1 = ((bf16[8,2,16,64,128]{4,3,2,1,0:T(8,128)(2,1)}), bf16[8,2,16,64,128]{4,3,2,1,0:T(8,128)(2,1)}, u32[]{:S(2)}, u32[]{:S(2)}) async-start(bf16[8,2,16,64,128]{4,3,2,1,0:T(8,128)(2,1)} %copy.13), calls=%async_computation.1 | async-start | bytes 8388608 | tf_op jit(solution)/shard_map/all_to_all | solution.py:30
Sparse Core Ops, SparseCore 0:
  13.6 41.4 all-gather.2

commit v2 on v0

--- a/solution.py
+++ b/solution.py
@@ -45,7 +45,9 @@
         scale_down, lax.axis_index(ZERO) * ready_down.shape[1], ready_down.shape[1], axis=1
     )
     part_router = (router_weight * router_gain[:, None]).astype(jnp.bfloat16)
-    row_router = lax.all_gather(part_router, ZERO, axis=0, tiled=True)
+    row_router = jnp.concatenate(
+        lax.all_to_all(jnp.stack([part_router] * lax.axis_size(ZERO)), ZERO, 0, 0), axis=0
+    )
     serve_router = lax.all_gather(row_router, "bank", axis=1, tiled=True)
     return (ready_down, scale_down, serve_router)
 

time: 209 us -> 200 us (0.957)
  blocking collectives: 124 us -> 20.7 us
  waiting for transfers between devices: 41.7 us -> 128 us
  starting transfers between devices: 4.71 us -> 9.25 us
  local copies, waits for them, and re-layouts: 11.6 us -> 14.8 us
    all_gather x1 -> x0, blocking collectives: 104 us -> none  [per_device(): row_router = lax.all_gather(part_router, ZERO, axis=0, tiled=True)]
    all_to_all x1, waiting for transfers between devices: 0.01 us -> 83.6 us  [turned_blocks(): lax.all_to_all(tiles, axes[k], split_axis=k, concat_axis=k, tiled=True)]
    all_to_all x0 -> x1, starting transfers between devices: none -> 4.36 us  [per_device(): lax.all_to_all(jnp.stack([part_router] * lax.axis_size(ZERO)), ZERO, 0, 0)]
    all_to_all x1, local copies, waits for them, and re-layouts: 2.97 us -> 5.52 us  [turned_blocks(): lax.all_to_all(tiles, axes[k], split_axis=k, concat_axis=k, tiled=True)]
    all_to_all x0 -> x1, waiting for transfers between devices: none -> 2.27 us  [per_device(): lax.all_to_all(jnp.stack([part_router] * lax.axis_size(ZERO)), ZERO, 0, 0)]
  transfers between devices with their start and end apart: 2 -> 3, of which waited for: 1 -> 3; matrix products, arithmetic and copies ran while one was open for 0% -> 3% of each run, Pallas kernels for 0% -> 0%
where the time goes in v2:
time: 200 us; the launch traced here: 199 us
  waiting for transfers between devices  128 us (64%)
  blocking collectives  20.7 us (10%)
  local copies, waits for them, and re-layouts  14.8 us (7%)
  between operations  14.2 us (7%)
  other arithmetic  12.8 us (6%)
  starting transfers between devices  9.25 us (5%)
    all_to_all x1, waiting for transfers between devices, turned_blocks(): lax.all_to_all(tiles, axes[k], split_axis=k, concat_axis=k, tiled=True)  83.6 us
    all_gather x1, waiting for transfers between devices, gathered_total(): tiles = lax.all_gather(value, axis)  41.6 us
    all_gather x1, blocking collectives, per_device(): serve_router = lax.all_gather(row_router, 'bank', axis=1, tiled=True)  12.5 us
    all_to_all x1, blocking collectives, turned_blocks(): lax.all_to_all(tiles, axes[k], split_axis=k, concat_axis=k, tiled=True)  8.15 us
    reduce_max x1, other arithmetic, per_device(): scale_down = gathered_total(jnp.max(jnp.abs(train_down), axis=2), ZERO)  6.25 us
    all_to_all x1, local copies, waits for them, and re-layouts, turned_blocks(): lax.all_to_all(tiles, axes[k], split_axis=k, concat_axis=k, tiled=True)  5.52 us
    reshape x1, local copies, waits for them, and re-layouts, joined_along(): tiles.reshape(*dims[:dim], dims[dim] * dims[dim + 1], *dims[dim + 2:])  5.35 us
    convert_element_type x1, other arithmetic, per_device(): (train_down / jnp.expand_dims(scale_down, 2)).astype(jnp.bfloat16)  5.26 us
  transfers between devices with their start and end apart: 3, of which 3 were waited for; matrix products, arithmetic and copies ran while one was open for 3% of the time, Pallas kernels for 0%

profile of v2, /device:TPU:2, one launch (start us, length us, event | category | flops | bytes accessed | tf_op | source)
XLA Modules:
  0.0 199.2 jit_solution(2524754201618451619)
XLA Ops:
  7.2 0.0 copy-start
  7.2 0.0 copy-start.1
  7.2 0.0 all-gather.3.cloned.1.call-start
  7.2 6.2 %abs_reduce_fusion = f32[16,1024]{1,0:T(8,128)} fusion(f32[16,1024,128]{2,1,0:T(8,128)} %param.3), kind=kLoop, calls=%fused_computation.1 | loop fusion | flops 4177920 | bytes 8454144 | tf_op jit(solution)/shard_map/reduce_max | solution.py:41
  13.5 0.0 all-gather.3.cloned.1.call-update
  13.5 0.0 copy-done
  13.5 0.0 copy-done.1
  13.5 41.6 %all-gather.3.cloned.1.call-done = f32[256,1024]{1,0:T(8,128)} async-done(((f32[16,1024]{1,0:T(8,128)}), f32[256,1024]{1,0:T(8,128)}) %all-gather.3.cloned.1.call-update) | async-done | bytes 1048592 | tf_op jit(solution)/shard_map/all_gather | solution.py:12
  55.2 1.3 reduce_max.19
  56.5 5.3 %divide_convert_fusion = bf16[16,1024,128]{2,1,0:T(8,128)(2,1)S(1)} fusion(f32[16,1024,128]{2,1,0:T(8,128)} %param.3, f32[16,1024]{1,0:T(8,128)S(1)} %reduce_max.19), kind=kLoop, calls=%fused_computation | loop fusion | flops 4194304 | bytes 12648448 | tf_op jit(solution)/shard_map/convert_element_type | solution.py:42
  62.4 1.3 copy.14
  63.7 8.2 %all_to_all.15 = bf16[8,2,16,64,128]{4,3,2,0,1:T(8,128)(2,1)} all-to-all(bf16[8,2,16,64,128]{4,3,2,0,1:T(8,128)(2,1)S(1)} %copy.14), channel_id=1, replica_groups=mesh['unit'=4,'bank'=4,'zero_0'=8,'zero_1'=2] {'zero_1'}, dimensions={1} | all-to-all | bytes 8388608 | tf_op jit(solution)/shard_map/all_to_all | solution.py:30
  71.9 0.6 stack.87
  72.5 4.4 %all-to-all-start.2 = ((bf16[16,128,16]{1,2,0:T(8,128)(2,1)}), bf16[16,128,16]{1,2,0:T(8,128)(2,1)S(1)}, u32[]{:S(2)}, u32[]{:S(2)}) async-start(bf16[16,128,16]{1,2,0:T(8,128)(2,1)} %stack.87), calls=%async_computation.2 | async-start | bytes 131072 | tf_op jit(solution)/shard_map/all_to_all | solution.py:49
  76.9 5.5 %copy.15 = bf16[8,2,16,64,128]{4,3,2,1,0:T(8,128)(2,1)} copy(bf16[8,2,16,64,128]{4,3,2,0,1:T(8,128)(2,1)} %all_to_all.15) | data formatting | bytes 8388608 | tf_op jit(solution)/shard_map/all_to_all | solution.py:30
  82.4 2.3 %all-to-all-done.2 = bf16[16,128,16]{1,2,0:T(8,128)(2,1)S(1)} async-done(((bf16[16,128,16]{1,2,0:T(8,128)(2,1)}), bf16[16,128,16]{1,2,0:T(8,128)(2,1)S(1)}, u32[]{:S(2)}, u32[]{:S(2)}) %all-to-all-start.2) | async-done | bytes 65568 | tf_op jit(solution)/shard_map/all_to_all | solution.py:49
  84.7 4.8 %all-to-all-start.1 = ((bf16[8,2,16,64,128]{4,3,2,1,0:T(8,128)(2,1)}), bf16[8,2,16,64,128]{4,3,2,1,0:T(8,128)(2,1)}, u32[]{:S(2)}, u32[]{:S(2)}) async-start(bf16[8,2,16,64,128]{4,3,2,1,0:T(8,128)(2,1)} %copy.15), calls=%async_computation.1 | async-start | bytes 8388608 | tf_op jit(solution)/shard_map/all_to_all | solution.py:30
  89.5 12.5 %all_gather.11 = bf16[2048,64]{0,1:T(8,128)(2,1)S(1)} all-gather(bf16[2048,16]{0,1:T(8,128)(2,1)S(1)} %copy_bitcast_fusion.1), channel_id=1, replica_groups=mesh['unit'=4,'bank'=4,'zero_0'=8,'zero_1'=2] {'bank'}, dimensions={1}, use_global_device_ids=true | all-gather | bytes 327680 | tf_op jit(solution)/shard_map/all_gather | solution.py:51
  102.0 0.7 constant_dynamic-slice_fusion
  102.7 83.6 %all-to-all-done.1 = bf16[8,2,16,64,128]{4,3,2,1,0:T(8,128)(2,1)} async-done(((bf16[8,2,16,64,128]{4,3,2,1,0:T(8,128)(2,1)}), bf16[8,2,16,64,128]{4,3,2,1,0:T(8,128)(2,1)}, u32[]{:S(2)}, u32[]{:S(2)}) %all-to-all-start.1) | async-done | bytes 4194336 | tf_op jit(solution)/shard_map/all_to_all | solution.py:30
  186.3 5.3 %copy.22 = bf16[16,16,8,8,128]{4,3,0,2,1:T(8,128)(2,1)} copy(bf16[16,16,8,8,128]{4,3,2,1,0:T(8,128)(2,1)} %bitcast.21) | data formatting | bytes 8388608 | tf_op jit(solution)/shard_map/reshape | solution.py:23
  191.7 0.7 copy.39
  (18 shorter events, 0.6 us)
Async XLA Ops:
  7.2 6.3 %copy-start = (f32[128,16]{0,1:T(8,128)S(1)}, f32[128,16]{0,1:T(8,128)}, u32[]{:S(2)}) copy-start(f32[128,16]{0,1:T(8,128)} %param.4) | copy-start | bytes 24580
  7.2 6.3 %copy-start.1 = (f32[128]{0:T(128)S(1)}, f32[128]{0:T(128)}, u32[]{:S(2)}) copy-start(f32[128]{0:T(128)} %param.5) | copy-start | bytes 1540
  7.2 48.0 %all-gather.3.cloned.1.call-start = ((), (), s32[]{:S(2)}) async-start(), calls=%async_computation.3 | async-start | bytes 1114112 | tf_op jit(solution)/shard_map/all_gather | solution.py:12
  72.5 12.2 %all-to-all-start.2 = ((bf16[16,128,16]{1,2,0:T(8,128)(2,1)}), bf16[16,128,16]{1,2,0:T(8,128)(2,1)S(1)}, u32[]{:S(2)}, u32[]{:S(2)}) async-start(bf16[16,128,16]{1,2,0:T(8,128)(2,1)} %stack.87), calls=%async_computation.2 | async-start | bytes 131072 | tf_op jit(solution)/shard_map/all_to_all | solution.py:49
  84.7 101.7 %all-to-all-start.1 = ((bf16[8,2,16,64,128]{4,3,2,1,0:T(8,128)(2,1)}), bf16[8,2,16,64,128]{4,3,2,1,0:T(8,128)(2,1)}, u32[]{:S(2)}, u32[]{:S(2)}) async-start(bf16[8,2,16,64,128]{4,3,2,1,0:T(8,128)(2,1)} %copy.15), calls=%async_computation.1 | async-start | bytes 8388608 | tf_op jit(solution)/shard_map/all_to_all | solution.py:30
Sparse Core Ops, SparseCore 0:
  13.6 41.4 all-gather.2
